TPU v7x, 32 devices: a whole 2x2x4 slice. The times are simulated.
32 devices in a mesh: dp: 8 (over z, y), mp: 4 (over x, core).
Axes of the slice: x: 2, y: 2, z: 4, core: 2. Of those that a mesh axis runs over, the one named last changes fastest.
Arguments:
- queries: bfloat16 [128, 8192], P('dp', 'mp'), may hold values from -8 to 8
- incoming_key: bfloat16 [128, 1024], P('dp', 'mp'), may hold values from -4 to 4
- incoming_value: bfloat16 [128, 1024], P('dp', 'mp'), may hold values from -4 to 4
- key_cache: bfloat16 [256, 256, 1024], P('dp', None, 'mp'), may hold values from -8 to 8
- cached_values: bfloat16 [256, 256, 1024], P('dp', None, 'mp'), may hold values from -4 to 4
- task_key_scale: bfloat16 [256, 1024], P(None, 'mp'), may hold values from 0.099609375 to 1.8984375
- task_value_scale: bfloat16 [256, 1024], P(None, 'mp'), may hold values from 0.099609375 to 1.8984375
- out_weight: bfloat16 [8192, 8192], P('mp', 'dp'), may hold values from -0.0625 to 0.0625
- task_id: int32 [128], P('dp'), may hold values from 0 to 255, as said below
- cached_length: int32 [128], P('dp'), may hold values from 1 to 256, as said below
- task_owner: int32 [256], replicated, may hold values from 0 to 7, as said below
- cache_slot: int32 [128], P('dp'), may hold values from 0 to 31, as said below
Outputs:
- layer_out: bfloat16 [128, 8192], P('dp', 'mp')
Inputs may be any that keep to these rules, and one draw needn't show every extreme that they name: `task_owner`: every dp index owns the same number of tasks. `task_id`: among the 16 requests of one dp index at most 4 have tasks of one owner; in every draw one owner gets exactly 4 from every dp index. `cache_slot`: requests of one owner have distinct slots; one owner uses all 32. `cached_length`: every dp index has a request with 256 cached positions.
All inputs are finite; a program needn't handle non-finite values.
Results may differ from a plain program's by a relative error of at most 0.0073.
Values may be sent and summed in bfloat16 or wider, within the bound.
A program may use at most 128 MiB of HBM per device.

v0:
```python
import math

import jax
import jax.numpy as jnp
from jax import lax
from jax.sharding import PartitionSpec as P

KEY_VALUE_HEADS = 8
HEAD_SIZE = 128
QUERY_HEADS = 64
MAX_POSITIONS = 256


masked_score = -1e30


def attend(queries, fresh_key_rows, fresh_value_rows, stored_key_rows, stored_value_rows, lengths):
    entry_count = queries.shape[0]
    kv_heads = fresh_key_rows.shape[1] // HEAD_SIZE
    group_width = QUERY_HEADS // KEY_VALUE_HEADS
    inv_root = 1.0 / math.sqrt(HEAD_SIZE)
    query_head_rows = queries.reshape(entry_count, kv_heads, group_width, HEAD_SIZE)
    previous_keys = stored_key_rows.reshape(entry_count, MAX_POSITIONS, kv_heads, HEAD_SIZE)
    previous_values = stored_value_rows.reshape(entry_count, MAX_POSITIONS, kv_heads, HEAD_SIZE)
    incoming_keys = fresh_key_rows.reshape(entry_count, kv_heads, HEAD_SIZE)
    incoming_values = fresh_value_rows.reshape(entry_count, kv_heads, HEAD_SIZE)
    scores = (
        jnp.einsum(
            "ngqd,njgd->ngqj", query_head_rows, previous_keys, preferred_element_type=jnp.float32
        )
        * inv_root
    )
    own_score = (
        jnp.einsum(
            "ngqd,ngd->ngq", query_head_rows, incoming_keys, preferred_element_type=jnp.float32
        )
        * inv_root
    )
    visible = (
        lax.broadcasted_iota(jnp.int32, (entry_count, 1, 1, MAX_POSITIONS), 3)
        < lengths[:, None, None, None]
    )
    scores = jnp.where(visible, scores, masked_score)
    top_score = jnp.maximum(jnp.max(scores, axis=3), own_score)
    weights = jnp.where(visible, jnp.exp(scores - top_score[..., None]), 0.0)
    own_weight = jnp.exp(own_score - top_score)
    weight_sum = jnp.sum(weights, axis=3) + own_weight
    blended = jnp.einsum(
        "ngqj,njgd->ngqd",
        weights.astype(jnp.bfloat16),
        previous_values,
        preferred_element_type=jnp.float32,
    )
    blended = (
        blended
        + own_weight.astype(jnp.bfloat16).astype(jnp.float32)[..., None]
        * incoming_values.astype(jnp.float32)[:, :, None, :]
    )
    return (
        (blended / weight_sum[..., None])
        .astype(jnp.bfloat16)
        .reshape(entry_count, kv_heads * group_width * HEAD_SIZE)
    )


def on_device(
    queries,
    incoming_key,
    incoming_value,
    key_cache,
    cached_values,
    task_key_scale,
    task_value_scale,
    out_weight,
    task_id,
    cached_length,
    task_owner,
    cache_slot,
):
    row_count = queries.shape[0]
    task_count = task_key_scale.shape[0]
    kv_width = incoming_key.shape[1]
    kv_heads = kv_width // HEAD_SIZE
    group_width = QUERY_HEADS // KEY_VALUE_HEADS
    owner_count = lax.axis_size("dp")
    capacity = 2 * row_count // owner_count
    picked = task_id[:, None] == lax.broadcasted_iota(jnp.int32, (row_count, task_count), 1)
    owner_of = jnp.sum(jnp.where(picked, task_owner[None, :], 0), axis=1)
    selector = picked.astype(jnp.bfloat16)
    key_factor = jnp.dot(selector, task_key_scale, preferred_element_type=jnp.float32)
    value_factor = jnp.dot(selector, task_value_scale, preferred_element_type=jnp.float32)
    scaled_rows = (
        (
            queries.astype(jnp.float32).reshape(row_count, kv_heads, group_width, HEAD_SIZE)
            * key_factor.reshape(row_count, kv_heads, 1, HEAD_SIZE)
        )
        .astype(jnp.bfloat16)
        .reshape(row_count, kv_heads * group_width * HEAD_SIZE)
    )
    head_width = scaled_rows.shape[1]
    earlier = lax.broadcasted_iota(jnp.int32, (row_count, row_count), 1) < lax.broadcasted_iota(
        jnp.int32, (row_count, row_count), 0
    )
    same_owner = owner_of[:, None] == owner_of[None, :]
    rank_in = jnp.sum(jnp.where(earlier & same_owner, 1, 0), axis=1)
    position = owner_of * capacity + rank_in
    slot_total = owner_count * capacity
    placing = position[None, :] == lax.broadcasted_iota(jnp.int32, (slot_total, row_count), 0)
    packer = placing.astype(jnp.bfloat16)
    unpacker = (
        position[:, None] == lax.broadcasted_iota(jnp.int32, (row_count, slot_total), 1)
    ).astype(jnp.bfloat16)

    def pack_rows(value_rows):
        packed = jnp.dot(packer, value_rows, preferred_element_type=jnp.float32).astype(
            jnp.bfloat16
        )
        return packed.reshape(owner_count, capacity, value_rows.shape[1])

    def pack_ints(value_rows):
        return (
            jnp.sum(jnp.where(placing, value_rows[None, :] + 1, 0), axis=1).reshape(
                owner_count, capacity
            )
            - 1
        )

    got_queries = lax.all_to_all(
        pack_rows(scaled_rows), "dp", split_axis=0, concat_axis=0, tiled=True
    )
    got_keys = lax.all_to_all(
        pack_rows(incoming_key), "dp", split_axis=0, concat_axis=0, tiled=True
    )
    got_values = lax.all_to_all(
        pack_rows(incoming_value), "dp", split_axis=0, concat_axis=0, tiled=True
    )
    slot_ids = lax.all_to_all(pack_ints(cache_slot), "dp", split_axis=0, concat_axis=0, tiled=True)
    got_lengths = lax.all_to_all(
        pack_ints(cached_length), "dp", split_axis=0, concat_axis=0, tiled=True
    )
    sources = slot_ids.shape[0]
    per_source = slot_ids.shape[1]
    item_total = sources * per_source
    flat_slots = jnp.maximum(slot_ids.reshape(item_total), 0)
    stored_key_rows = jnp.take(key_cache, flat_slots, axis=0)
    stored_value_rows = jnp.take(cached_values, flat_slots, axis=0)
    result = attend(
        got_queries.reshape(item_total, head_width),
        got_keys.reshape(item_total, kv_width),
        got_values.reshape(item_total, kv_width),
        stored_key_rows,
        stored_value_rows,
        got_lengths.reshape(item_total),
    )
    answered = result.reshape(sources, per_source, head_width)
    returned = lax.all_to_all(answered, "dp", split_axis=0, concat_axis=0, tiled=True)
    attention_output = jnp.dot(
        unpacker, returned.reshape(slot_total, head_width), preferred_element_type=jnp.float32
    ).astype(jnp.bfloat16)
    context_rows = (
        (
            attention_output.astype(jnp.float32).reshape(
                row_count, kv_heads, group_width, HEAD_SIZE
            )
            * value_factor.reshape(row_count, kv_heads, 1, HEAD_SIZE)
        )
        .astype(jnp.bfloat16)
        .reshape(row_count, head_width)
    )
    partial_value = jnp.dot(
        context_rows,
        lax.all_gather(out_weight, "dp", axis=1, tiled=True),
        preferred_element_type=jnp.float32,
    )
    return lax.psum_scatter(partial_value, "mp", scatter_dimension=1, tiled=True).astype(
        jnp.bfloat16
    )


def solution(mesh):
    placed = (
        P("dp", "mp"),
        P("dp", "mp"),
        P("dp", "mp"),
        P("dp", None, "mp"),
        P("dp", None, "mp"),
        P(None, "mp"),
        P(None, "mp"),
        P("mp", "dp"),
        P("dp"),
        P("dp"),
        P(),
        P("dp"),
    )
    return jax.shard_map(
        on_device, mesh=mesh, in_specs=placed, out_specs=P("dp", "mp"), check_vma=False
    )
```

profile of v0, /device:TPU:0, one launch (start us, length us, event | category | flops | bytes accessed | tf_op | source)
XLA Modules:
  0.0 696.8 jit_solution(11836538279742100467)
XLA Ops:
  6.6 0.7 all-gather.2.cloned.1.call-update
  7.9 0.7 sub.24
  8.5 7.3 %all-to-all-start.2 = ((s32[8,1,4]{2,1,0:T(1,128)}), s32[8,1,4]{2,1,0:T(1,128)S(1)}, u32[]{:S(2)}, u32[]{:S(2)}) async-start(s32[8,1,4]{2,1,0:T(1,128)} %bitcast.1), calls=%async_computation.2 | async-start | bytes 8192 | tf_op jit(solution)/shard_map/all_to_all | solution.py:137
  16.6 0.3 convolution_convert_fusion
  16.9 0.7 sub.22
  17.6 0.7 reshape.119
  18.3 0.6 reshape.121
  18.9 0.6 reshape.123
  19.5 2.8 all-to-all-done.2
  22.3 3.3 all-to-all-start
  25.7 42.1 %all-to-all-done = s32[8,1,4]{2,1,0:T(1,128)S(1)} async-done(((s32[8,1,4]{2,1,0:T(1,128)}), s32[8,1,4]{2,1,0:T(1,128)S(1)}, u32[]{:S(2)}, u32[]{:S(2)}) %all-to-all-start) | async-done | bytes 160 | tf_op jit(solution)/shard_map/all_to_all | solution.py:138
  67.8 3.3 all-to-all-start.3
  71.2 6.6 all-to-all-done.3
  77.8 3.3 all-to-all-start.4
  81.2 5.1 gather_fusion
  86.3 5.0 gather_fusion.1
  91.3 0.9 all-to-all-done.4
  92.2 4.9 all-to-all-start.1
  97.1 5.9 select_bitcast_fusion.1
  103.0 0.5 broadcast.82
  103.5 0.7 reduce.7
  104.4 1.5 all-to-all-done.1
  106.2 3.6 fusion.47
  109.9 0.3 fusion.25
  110.2 0.7 fusion.21
  111.0 0.7 reshape_reshape.12
  111.7 11.8 %all-to-all-start.5 = ((bf16[8,4,2048]{2,1,0:T(4,128)(2,1)}), bf16[8,4,2048]{2,1,0:T(4,128)(2,1)S(1)}, u32[]{:S(2)}, u32[]{:S(2)}) async-start(bf16[8,4,2048]{2,1,0:T(4,128)(2,1)} %reshape_reshape.12), calls=%async_computation.5 | async-start | bytes 262144 | tf_op jit(solution)/shard_map/all_to_all | solution.py:156
  123.7 9.0 %all-to-all-done.5 = bf16[8,4,2048]{2,1,0:T(4,128)(2,1)S(1)} async-done(((bf16[8,4,2048]{2,1,0:T(4,128)(2,1)}), bf16[8,4,2048]{2,1,0:T(4,128)(2,1)S(1)}, u32[]{:S(2)}, u32[]{:S(2)}) %all-to-all-start.5) | async-done | bytes 131104 | tf_op jit(solution)/shard_map/all_to_all | solution.py:156
  132.7 520.1 %all-gather.2.cloned.1.call-done = bf16[2048,8192]{1,0:T(8,128)(2,1)} async-done(((bf16[2048,1024]{1,0:T(8,128)(2,1)}), bf16[2048,8192]{1,0:T(8,128)(2,1)}) %all-gather.2.cloned.1.call-update) | async-done | bytes 33554448 | tf_op jit(solution)/shard_map/all_gather | solution.py:172
  652.8 13.8 %fusion.24 = f32[16,8192]{1,0:T(8,128)} fusion(bf16[2048,8192]{1,0:T(8,128)(2,1)} %all-gather.2.cloned.1.call-done, bf16[32,2048]{1,0:T(8,128)(2,1)S(1)} %reshape.124, f32[2,8,16,128]{3,2,1,0:T(8,128)S(1)} %bitcast.51, s32[16]{0:T(128)S(1)} %multiply_add_fusion), kind=kOutput, calls=%fused_computation.22 | convolution fusion | flops 539099648 | bytes 34340928 | tf_op jit(solution)/shard_map/dot_general | solution.py:170
  666.7 21.7 %reduce-scatter.2.cloned.1.call-done = f32[16,2048]{1,0:T(8,128)} async-done(((f32[16,8192]{1,0:T(8,128)}), f32[16,2048]{1,0:T(8,128)}) %reduce-scatter.2.cloned.1.call-update) | async-done | bytes 131088 | tf_op jit(solution)/shard_map/reduce_scatter | solution.py:175
  688.4 1.5 convert_element_type.68
  (52 shorter events, 2.2 us)
Async XLA Ops:
  6.5 9.3 %copy-start = (bf16[256,256]{1,0:T(8,128)(2,1)S(1)}, bf16[256,256]{1,0:T(8,128)(2,1)}, u32[]{:S(2)}) copy-start(bf16[256,256]{1,0:T(8,128)(2,1)} %param.19) | copy-start | bytes 393220
  6.5 0.8 copy-start.4
  6.5 0.8 copy-start.3
  6.5 1.2 copy-start.8
  6.5 1.2 copy-start.9
  6.5 9.5 %copy-start.6 = (bf16[16,256]{1,0:T(8,128)(2,1)S(1)}, bf16[16,256]{1,0:T(8,128)(2,1)}, u32[]{:S(2)}) copy-start(bf16[16,256]{1,0:T(8,128)(2,1)} %param.15) | copy-start | bytes 24580
  6.6 9.8 %copy-start.7 = (bf16[16,256]{1,0:T(8,128)(2,1)S(1)}, bf16[16,256]{1,0:T(8,128)(2,1)}, u32[]{:S(2)}) copy-start(bf16[16,256]{1,0:T(8,128)(2,1)} %param.16) | copy-start | bytes 24580
  6.6 10.0 %copy-start.2 = (bf16[16,2048]{1,0:T(8,128)(2,1)S(1)}, bf16[16,2048]{1,0:T(8,128)(2,1)}, u32[]{:S(2)}) copy-start(bf16[16,2048]{1,0:T(8,128)(2,1)} %param.14) | copy-start | bytes 196612
  6.6 646.2 %all-gather.2.cloned.1.call-start = ((), (), s32[]{:S(2)}) async-start(), calls=%async_computation.7 | async-start | bytes 37748736 | tf_op jit(solution)/shard_map/all_gather | solution.py:172
  8.5 13.8 %all-to-all-start.2 = ((s32[8,1,4]{2,1,0:T(1,128)}), s32[8,1,4]{2,1,0:T(1,128)S(1)}, u32[]{:S(2)}, u32[]{:S(2)}) async-start(s32[8,1,4]{2,1,0:T(1,128)} %bitcast.1), calls=%async_computation.2 | async-start | bytes 8192 | tf_op jit(solution)/shard_map/all_to_all | solution.py:137
  22.3 45.5 %all-to-all-start = ((s32[8,1,4]{2,1,0:T(1,128)}), s32[8,1,4]{2,1,0:T(1,128)S(1)}, u32[]{:S(2)}, u32[]{:S(2)}) async-start(s32[8,1,4]{2,1,0:T(1,128)} %bitcast), calls=%async_computation | async-start | bytes 8192 | tf_op jit(solution)/shard_map/all_to_all | solution.py:138
  67.8 10.0 %all-to-all-start.3 = ((bf16[8,4,256]{2,1,0:T(4,128)(2,1)}), bf16[8,4,256]{2,1,0:T(4,128)(2,1)S(1)}, u32[]{:S(2)}, u32[]{:S(2)}) async-start(bf16[8,4,256]{2,1,0:T(4,128)(2,1)} %reshape.121), calls=%async_computation.3 | async-start | bytes 32768 | tf_op jit(solution)/shard_map/all_to_all | solution.py:131
  77.8 14.4 %all-to-all-start.4 = ((bf16[8,4,256]{2,1,0:T(4,128)(2,1)}), bf16[8,4,256]{2,1,0:T(4,128)(2,1)S(1)}, u32[]{:S(2)}, u32[]{:S(2)}) async-start(bf16[8,4,256]{2,1,0:T(4,128)(2,1)} %reshape.123), calls=%async_computation.4 | async-start | bytes 32768 | tf_op jit(solution)/shard_map/all_to_all | solution.py:134
  92.2 13.7 %all-to-all-start.1 = ((bf16[8,4,2048]{2,1,0:T(4,128)(2,1)}), bf16[8,4,2048]{2,1,0:T(4,128)(2,1)S(1)}, u32[]{:S(2)}, u32[]{:S(2)}) async-start(bf16[8,4,2048]{2,1,0:T(4,128)(2,1)} %reshape.119), calls=%async_computation.1 | async-start | bytes 262144 | tf_op jit(solution)/shard_map/all_to_all | solution.py:128
  106.0 4.3 copy-start.1
  109.9 13.6 %copy-start.5 = (bf16[256,256]{1,0:T(8,128)(2,1)S(1)}, bf16[256,256]{1,0:T(8,128)(2,1)}, u32[]{:S(2)}) copy-start(bf16[256,256]{1,0:T(8,128)(2,1)} %param.20) | copy-start | bytes 393220
  111.7 21.0 %all-to-all-start.5 = ((bf16[8,4,2048]{2,1,0:T(4,128)(2,1)}), bf16[8,4,2048]{2,1,0:T(4,128)(2,1)S(1)}, u32[]{:S(2)}, u32[]{:S(2)}) async-start(bf16[8,4,2048]{2,1,0:T(4,128)(2,1)} %reshape_reshape.12), calls=%async_computation.5 | async-start | bytes 262144 | tf_op jit(solution)/shard_map/all_to_all | solution.py:156
  123.4 565.0 %reduce-scatter.2.cloned.1.call-start = ((), (), s32[]{:S(2)}) async-start(), calls=%async_computation.8 | async-start | bytes 655360 | tf_op jit(solution)/shard_map/reduce_scatter | solution.py:175
Sparse Core Ops, SparseCore 0:
  8.9 643.8 all-gather.1
  666.8 21.5 reduce-scatter.1
where the time goes:
time: 697 us
  waiting for transfers between devices  606 us (87%)
  starting transfers between devices  34 us (5%)
  matrix products  19.6 us (3%)
  local copies, waits for them, and re-layouts  15 us (2%)
  between operations  13.7 us (2%)
  other arithmetic  9.1 us (1%)
    all_gather x1, waiting for transfers between devices, on_device(): lax.all_gather(out_weight, 'dp', axis=1, tiled=True)  520 us
    all_to_all x1, waiting for transfers between devices, on_device(): lax.all_to_all(pack_ints(cached_length), 'dp', split_axis=0, concat_axis=...  42.1 us
    reduce_scatter x1, waiting for transfers between devices, on_device(): lax.psum_scatter(partial_value, 'mp', scatter_dimension=1, tiled=True)  21.7 us
  transfers between devices with their start and end apart: 8, of which 8 were waited for; matrix products, arithmetic and copies ran while one was open for 4% of the time, Pallas kernels for 0%

commit v1 on v0

--- a/solution.py
+++ b/solution.py
@@ -167,14 +167,14 @@
         .astype(jnp.bfloat16)
         .reshape(row_count, head_width)
     )
-    partial_value = jnp.dot(
-        context_rows,
-        lax.all_gather(out_weight, "dp", axis=1, tiled=True),
-        preferred_element_type=jnp.float32,
-    )
-    return lax.psum_scatter(partial_value, "mp", scatter_dimension=1, tiled=True).astype(
+    all_rows = lax.all_gather(context_rows, "dp", axis=0, tiled=True)
+    partial_value = jnp.dot(all_rows, out_weight, preferred_element_type=jnp.float32).astype(
         jnp.bfloat16
     )
+    own_rows = lax.all_to_all(partial_value, "dp", split_axis=0, concat_axis=1, tiled=True)
+    return lax.psum_scatter(
+        own_rows.astype(jnp.float32), "mp", scatter_dimension=1, tiled=True
+    ).astype(jnp.bfloat16)
 
 
 def solution(mesh):

time: 697 us -> 167 us (0.24)
  waiting for transfers between devices: 606 us -> 40.2 us
  blocking collectives: 0 us -> 42.4 us
  matrix products: 19.6 us -> 11.8 us
    all_gather x1 -> x0, waiting for transfers between devices: 520 us -> none  [on_device(): lax.all_gather(out_weight, 'dp', axis=1, tiled=True)]
    all_to_all x1, waiting for transfers between devices: 42.1 us -> 6.39 us  [on_device(): lax.all_to_all(pack_ints(cached_length), 'dp', split_axis=0, concat_axis=...]
    all_gather x0 -> x1, blocking collectives: none -> 31.8 us  [on_device(): all_rows = lax.all_gather(context_rows, 'dp', axis=0, tiled=True)]
    dot_general x1 -> x2, matrix products: 13.8 us -> 3.16 us  [the longest x1 2.95 us: on_device(): jnp.dot(all_rows, out_weight, preferred_element_type=jnp.float32)]
    all_to_all x0 -> x1, blocking collectives: none -> 10.6 us  [on_device(): lax.all_to_all(partial_value, 'dp', split_axis=0, concat_axis=1, tiled=True)]
  transfers between devices with their start and end apart: 8 -> 7, of which waited for: 8 -> 5; matrix products, arithmetic and copies ran while one was open for 4% -> 14% of each run, Pallas kernels for 0% -> 0%
where the time goes in v1:
time: 167 us
  blocking collectives  42.4 us (25%)
  waiting for transfers between devices  40.2 us (24%)
  starting transfers between devices  31.9 us (19%)
  local copies, waits for them, and re-layouts  15.6 us (9%)
  between operations  13.6 us (8%)
  matrix products  11.8 us (7%)
  other arithmetic  11.1 us (7%)
    all_gather x1, blocking collectives, on_device(): all_rows = lax.all_gather(context_rows, 'dp', axis=0, tiled=True)  31.8 us
    reduce_scatter x1, waiting for transfers between devices, on_device(): lax.psum_scatter(own_rows.astype(jnp.float32), 'mp', scatter_dimension=1,...  20.2 us
    all_to_all x1, blocking collectives, on_device(): lax.all_to_all(partial_value, 'dp', split_axis=0, concat_axis=1, tiled=True)  10.6 us
    all_to_all x1, starting transfers between devices, on_device(): lax.all_to_all(pack_ints(cache_slot), 'dp', split_axis=0, concat_axis=0,...  7.31 us
    all_to_all x1, waiting for transfers between devices, on_device(): lax.all_to_all(answered, 'dp', split_axis=0, concat_axis=0, tiled=True)  7.08 us
    all_to_all x1, waiting for transfers between devices, on_device(): lax.all_to_all(pack_rows(incoming_key), 'dp', split_axis=0, concat_axis=0...  6.5 us
    all_to_all x1, waiting for transfers between devices, on_device(): lax.all_to_all(pack_ints(cached_length), 'dp', split_axis=0, concat_axis=...  6.39 us
    all_to_all x1, starting transfers between devices, on_device(): lax.all_to_all(pack_ints(cached_length), 'dp', split_axis=0, concat_axis=...  5.99 us
  transfers between devices with their start and end apart: 7, of which 5 were waited for; matrix products, arithmetic and copies ran while one was open for 14% of the time, Pallas kernels for 0%

profile of v1, /device:TPU:0, one launch (start us, length us, event | category | flops | bytes accessed | tf_op | source)
XLA Modules:
  0.0 166.6 jit_solution(14488211424720832008)
XLA Ops:
  6.5 0.9 select_reduce_fusion
  7.6 0.7 broadcast_add_fusion.2
  8.3 0.7 broadcast_add_fusion.3
  9.1 0.7 sub.24
  9.7 7.3 %all-to-all-start.2 = ((s32[8,1,4]{2,1,0:T(1,128)}), s32[8,1,4]{2,1,0:T(1,128)S(1)}, u32[]{:S(2)}, u32[]{:S(2)}) async-start(s32[8,1,4]{2,1,0:T(1,128)} %bitcast.1), calls=%async_computation.2 | async-start | bytes 8192 | tf_op jit(solution)/shard_map/all_to_all | solution.py:137
  17.0 0.8 fusion.33
  17.9 1.0 convolution_convert_fusion.4
  18.9 1.0 convolution_convert_fusion.3
  19.8 1.1 convolution_convert_fusion
  21.0 0.7 sub.22
  21.6 0.7 reshape.124
  23.6 6.0 %all-to-all-start = ((s32[8,1,4]{2,1,0:T(1,128)}), s32[8,1,4]{2,1,0:T(1,128)S(1)}, u32[]{:S(2)}, u32[]{:S(2)}) async-start(s32[8,1,4]{2,1,0:T(1,128)} %bitcast), calls=%async_computation | async-start | bytes 8192 | tf_op jit(solution)/shard_map/all_to_all | solution.py:138
  29.7 6.4 %all-to-all-done = s32[8,1,4]{2,1,0:T(1,128)S(1)} async-done(((s32[8,1,4]{2,1,0:T(1,128)}), s32[8,1,4]{2,1,0:T(1,128)S(1)}, u32[]{:S(2)}, u32[]{:S(2)}) %all-to-all-start) | async-done | bytes 160 | tf_op jit(solution)/shard_map/all_to_all | solution.py:138
  36.1 3.3 %all-to-all-start.3 = ((bf16[8,4,256]{2,1,0:T(4,128)(2,1)}), bf16[8,4,256]{2,1,0:T(4,128)(2,1)S(1)}, u32[]{:S(2)}, u32[]{:S(2)}) async-start(bf16[8,4,256]{2,1,0:T(4,128)(2,1)} %reshape.126), calls=%async_computation.3 | async-start | bytes 32768 | tf_op jit(solution)/shard_map/all_to_all | solution.py:131
  39.4 6.5 %all-to-all-done.3 = bf16[8,4,256]{2,1,0:T(4,128)(2,1)S(1)} async-done(((bf16[8,4,256]{2,1,0:T(4,128)(2,1)}), bf16[8,4,256]{2,1,0:T(4,128)(2,1)S(1)}, u32[]{:S(2)}, u32[]{:S(2)}) %all-to-all-start.3) | async-done | bytes 16416 | tf_op jit(solution)/shard_map/all_to_all | solution.py:131
  45.9 3.3 %all-to-all-start.4 = ((bf16[8,4,256]{2,1,0:T(4,128)(2,1)}), bf16[8,4,256]{2,1,0:T(4,128)(2,1)S(1)}, u32[]{:S(2)}, u32[]{:S(2)}) async-start(bf16[8,4,256]{2,1,0:T(4,128)(2,1)} %reshape.128), calls=%async_computation.4 | async-start | bytes 32768 | tf_op jit(solution)/shard_map/all_to_all | solution.py:134
  49.2 4.9 %gather_fusion = bf16[32,256,256]{2,1,0:T(8,128)(2,1)} fusion(bf16[32,256,256]{2,1,0:T(8,128)(2,1)} %param.17, s32[1024]{0:T(1024)S(1)} %pad_clamp_fusion), kind=kCustom, calls=%fused_computation.clone | custom fusion | bytes 8388736 | tf_op jit(solution)/shard_map/jit(_take)/gather | solution.py:145
  54.2 5.0 %gather_fusion.1 = bf16[32,256,256]{2,1,0:T(8,128)(2,1)} fusion(bf16[32,256,256]{2,1,0:T(8,128)(2,1)} %param.18, s32[1024]{0:T(1024)S(1)} %pad_clamp_fusion), kind=kCustom, calls=%fused_computation.1.clone | custom fusion | bytes 8388736 | tf_op jit(solution)/shard_map/jit(_take)/gather | solution.py:146
  59.2 5.9 %all-to-all-start.1 = ((bf16[8,4,2048]{2,1,0:T(4,128)(2,1)}), bf16[8,4,2048]{2,1,0:T(4,128)(2,1)S(1)}, u32[]{:S(2)}, u32[]{:S(2)}) async-start(bf16[8,4,2048]{2,1,0:T(4,128)(2,1)} %reshape.124), calls=%async_computation.1 | async-start | bytes 262144 | tf_op jit(solution)/shard_map/all_to_all | solution.py:128
  65.1 5.9 %select_bitcast_fusion.1 = (bf16[32,32,2,8,128]{4,3,2,1,0:T(8,128)(2,1)}, bf16[32,32,2,8,128]{4,3,2,1,0:T(8,128)(2,1)}) fusion(bf16[32,256,256]{2,1,0:T(8,128)(2,1)} %gather_fusion, pred[32]{0:T(512)(128)(4,1)S(1)} %compare_and_fusion, bf16[32,256,256]{2,1,0:T(8,128)(2,1)} %gather_fusion.1), kind=kLoop, calls=%fused_computation.9 | loop fusion | flops 4194304 | bytes 16777248
  71.5 0.7 reduce.7
  72.7 3.6 %fusion.43 = (f32[32,2,8]{2,1,0:T(2,128)S(1)}, f32[32,2,8,256]{3,2,1,0:T(8,128)S(1)}) fusion(bf16[32,2,8,128]{3,2,1,0:T(8,128)(2,1)S(1)} %reshape_reshape.10, bf16[32,32,2,8,128]{4,3,2,1,0:T(8,128)(2,1)} %get-tuple-element.10, pred[32,256]{1,0:T(8,128)(4,1)S(1)} %iota_compare_fusion), kind=kOutput, calls=%fused_computation.64 | convolution fusion | flops 33947136 | bytes 4859904 | tf_op jit(solution)/shard_map/ngqd,njgd->ngqj/dot_general | solution.py:28
  76.8 0.7 fusion.21
  77.5 0.7 reshape_reshape.12
  78.2 5.9 %all-to-all-start.5 = ((bf16[8,4,2048]{2,1,0:T(4,128)(2,1)}), bf16[8,4,2048]{2,1,0:T(4,128)(2,1)S(1)}, u32[]{:S(2)}, u32[]{:S(2)}) async-start(bf16[8,4,2048]{2,1,0:T(4,128)(2,1)} %reshape_reshape.12), calls=%async_computation.5 | async-start | bytes 262144 | tf_op jit(solution)/shard_map/all_to_all | solution.py:156
  84.4 7.1 %all-to-all-done.5 = bf16[8,4,2048]{2,1,0:T(4,128)(2,1)S(1)} async-done(((bf16[8,4,2048]{2,1,0:T(4,128)(2,1)}), bf16[8,4,2048]{2,1,0:T(4,128)(2,1)S(1)}, u32[]{:S(2)}, u32[]{:S(2)}) %all-to-all-start.5) | async-done | bytes 131104 | tf_op jit(solution)/shard_map/all_to_all | solution.py:156
  91.8 31.8 %all_gather.3 = bf16[128,2048]{1,0:T(8,128)(2,1)S(1)} all-gather(bf16[16,2048]{1,0:T(8,128)(2,1)S(1)} %fusion.8), channel_id=1, replica_groups=mesh['dp'=8,'mp'=4] {'dp'}, dimensions={0}, use_global_device_ids=true | all-gather | bytes 589824 | tf_op jit(solution)/shard_map/all_gather | solution.py:170
  123.5 3.0 %convolution_convert_fusion.2 = bf16[128,1024]{1,0:T(8,128)(2,1)S(1)} fusion(bf16[128,2048]{1,0:T(8,128)(2,1)S(1)} %all_gather.3, bf16[2048,1024]{1,0:T(8,128)(2,1)} %param.21), kind=kOutput, calls=%fused_computation.17 | convolution fusion | flops 537001984 | bytes 4980736 | tf_op jit(solution)/shard_map/dot_general | solution.py:171
  126.5 10.6 %all_to_all.45 = bf16[8,16,1024]{2,1,0:T(8,128)(2,1)S(1)} all-to-all(bf16[8,16,1024]{2,1,0:T(8,128)(2,1)S(1)} %bitcast.55), channel_id=1, replica_groups=mesh['dp'=8,'mp'=4] {'dp'}, dimensions={0} | all-to-all | bytes 524288 | tf_op jit(solution)/shard_map/all_to_all | solution.py:174
  137.2 0.8 copy.33
  138.0 20.2 %reduce-scatter.2.cloned.1.call-done = f32[16,2048]{1,0:T(8,128)} async-done(((f32[16,8192]{1,0:T(8,128)}), f32[16,2048]{1,0:T(8,128)}) %reduce-scatter.2.cloned.1.call-update) | async-done | bytes 131088 | tf_op jit(solution)/shard_map/reduce_scatter | solution.py:175
  158.2 1.5 convert_element_type.84
  (42 shorter events, 3.7 us)
Async XLA Ops:
  6.5 10.5 %copy-start = (bf16[256,256]{1,0:T(8,128)(2,1)S(1)}, bf16[256,256]{1,0:T(8,128)(2,1)}, u32[]{:S(2)}) copy-start(bf16[256,256]{1,0:T(8,128)(2,1)} %param.19) | copy-start | bytes 393220
  9.7 13.8 %all-to-all-start.2 = ((s32[8,1,4]{2,1,0:T(1,128)}), s32[8,1,4]{2,1,0:T(1,128)S(1)}, u32[]{:S(2)}, u32[]{:S(2)}) async-start(s32[8,1,4]{2,1,0:T(1,128)} %bitcast.1), calls=%async_computation.2 | async-start | bytes 8192 | tf_op jit(solution)/shard_map/all_to_all | solution.py:137
  23.6 12.5 %all-to-all-start = ((s32[8,1,4]{2,1,0:T(1,128)}), s32[8,1,4]{2,1,0:T(1,128)S(1)}, u32[]{:S(2)}, u32[]{:S(2)}) async-start(s32[8,1,4]{2,1,0:T(1,128)} %bitcast), calls=%async_computation | async-start | bytes 8192 | tf_op jit(solution)/shard_map/all_to_all | solution.py:138
  36.1 9.9 %all-to-all-start.3 = ((bf16[8,4,256]{2,1,0:T(4,128)(2,1)}), bf16[8,4,256]{2,1,0:T(4,128)(2,1)S(1)}, u32[]{:S(2)}, u32[]{:S(2)}) async-start(bf16[8,4,256]{2,1,0:T(4,128)(2,1)} %reshape.126), calls=%async_computation.3 | async-start | bytes 32768 | tf_op jit(solution)/shard_map/all_to_all | solution.py:131
  45.9 13.2 %all-to-all-start.4 = ((bf16[8,4,256]{2,1,0:T(4,128)(2,1)}), bf16[8,4,256]{2,1,0:T(4,128)(2,1)S(1)}, u32[]{:S(2)}, u32[]{:S(2)}) async-start(bf16[8,4,256]{2,1,0:T(4,128)(2,1)} %reshape.128), calls=%async_computation.4 | async-start | bytes 32768 | tf_op jit(solution)/shard_map/all_to_all | solution.py:134
  59.2 13.3 %all-to-all-start.1 = ((bf16[8,4,2048]{2,1,0:T(4,128)(2,1)}), bf16[8,4,2048]{2,1,0:T(4,128)(2,1)S(1)}, u32[]{:S(2)}, u32[]{:S(2)}) async-start(bf16[8,4,2048]{2,1,0:T(4,128)(2,1)} %reshape.124), calls=%async_computation.1 | async-start | bytes 262144 | tf_op jit(solution)/shard_map/all_to_all | solution.py:128
  72.5 4.3 %copy-start.1 = (bf16[32,32,2,8,128]{4,3,2,1,0:T(8,128)(2,1)S(1)}, bf16[32,32,2,8,128]{4,3,2,1,0:T(8,128)(2,1)}, u32[]{:S(2)}) copy-start(bf16[32,32,2,8,128]{4,3,2,1,0:T(8,128)(2,1)} %get-tuple-element.11) | copy-start | bytes 12582916
  76.4 7.8 %copy-start.2 = (s32[16]{0:T(128)S(1)}, s32[16]{0:T(128)}, u32[]{:S(2)}) copy-start(s32[16]{0:T(128)} %param.22) | copy-start | bytes 196
  76.4 7.8 %copy-start.3 = (bf16[256,256]{1,0:T(8,128)(2,1)S(1)}, bf16[256,256]{1,0:T(8,128)(2,1)}, u32[]{:S(2)}) copy-start(bf16[256,256]{1,0:T(8,128)(2,1)} %param.20) | copy-start | bytes 393220
  78.2 13.3 %all-to-all-start.5 = ((bf16[8,4,2048]{2,1,0:T(4,128)(2,1)}), bf16[8,4,2048]{2,1,0:T(4,128)(2,1)S(1)}, u32[]{:S(2)}, u32[]{:S(2)}) async-start(bf16[8,4,2048]{2,1,0:T(4,128)(2,1)} %reshape_reshape.12), calls=%async_computation.5 | async-start | bytes 262144 | tf_op jit(solution)/shard_map/all_to_all | solution.py:156
  84.2 74.0 %reduce-scatter.2.cloned.1.call-start = ((), (), s32[]{:S(2)}) async-start(), calls=%async_computation.8 | async-start | bytes 655360 | tf_op jit(solution)/shard_map/reduce_scatter | solution.py:175
Sparse Core Ops, SparseCore 0:
  138.1 20.0 reduce-scatter.1

commit v2 on v1

v2 whole, which is shorter than its diff:
```python
import functools
import math

import jax
import jax.numpy as jnp
from jax import lax
from jax.experimental import pallas as pl
from jax.experimental.pallas import tpu as pltpu
from jax.sharding import PartitionSpec as P

KEY_VALUE_HEADS = 8
HEAD_SIZE = 128
QUERY_HEADS = 64
GROUP = QUERY_HEADS // KEY_VALUE_HEADS
META = 128
FIRST = 16
MESH = pl.DeviceIdType.MESH

masked_score = -1e30
f32 = jnp.float32
bf16 = jnp.bfloat16


def iota(shape, dim):
    return lax.broadcasted_iota(jnp.int32, shape, dim)


def to_column(row):
    n = row.shape[1]
    eye = iota((n, n), 0) == iota((n, n), 1)
    return jnp.sum(jnp.where(eye, row, 0.0), axis=1, keepdims=True)


def to_row(column):
    n = column.shape[0]
    eye = iota((n, n), 0) == iota((n, n), 1)
    return jnp.sum(jnp.where(eye, column, 0.0), axis=0, keepdims=True)


def dot(a, b):
    return jnp.dot(a, b, preferred_element_type=f32)


def layer_kernel(
    dp,
    mp,
    query_ref,
    new_key_ref,
    new_value_ref,
    key_scale_ref,
    value_scale_ref,
    task_ref,
    length_ref,
    slot_ref,
    owner_ref,
    key_hbm,
    value_hbm,
    weight_hbm,
    out_ref,
    keys,
    values,
    weight,
    rows_f32,
    send_rows,
    recv_rows,
    slot_query,
    slot_small,
    slot_length,
    slot_context,
    context,
    selector,
    send_part,
    recv_part,
    local_sem,
    send_sem,
    recv_sem,
):
    me = lax.axis_index("dp")
    part = lax.axis_index("mp")
    rows, query_width = query_ref.shape
    kv_width = new_key_ref.shape[1]
    kv_heads = kv_width // HEAD_SIZE
    heads = kv_heads * GROUP
    task_total = key_scale_ref.shape[0]
    slots, positions, _ = keys.shape
    capacity = send_rows.shape[1]
    items = dp * capacity
    columns = weight.shape[1]
    blocks = dp // mp
    meta_at = query_width + 2 * kv_width

    total = dp * mp
    here = me * mp + part
    barrier = pltpu.get_barrier_semaphore()

    def greet(k, carry):
        other = lax.rem(here + k, total)
        pl.semaphore_signal(
            barrier,
            inc=1,
            device_id=(other // mp, lax.rem(other, mp)),
            device_id_type=MESH,
        )
        return carry

    lax.fori_loop(1, total, greet, 0)

    fetches = [
        pltpu.make_async_copy(key_hbm, keys, local_sem.at[0]),
        pltpu.make_async_copy(value_hbm, values, local_sem.at[1]),
        pltpu.make_async_copy(weight_hbm, weight, local_sem.at[2]),
    ]
    for fetch in fetches:
        fetch.start()

    task_column = to_column(task_ref[...].astype(f32))
    length_column = to_column(length_ref[...].astype(f32))
    slot_column = to_column(slot_ref[...].astype(f32))
    picked = task_column == iota((rows, task_total), 1).astype(f32)
    owner_column = jnp.sum(
        jnp.where(picked, owner_ref[...].astype(f32), 0.0), axis=1, keepdims=True
    )
    owner_row = to_row(owner_column)
    earlier = iota((rows, rows), 1) < iota((rows, rows), 0)
    rank = jnp.sum(
        jnp.where(earlier & (owner_column == owner_row), 1.0, 0.0), axis=1, keepdims=True
    )
    position_row = to_row(owner_column * capacity + rank)
    packer = jnp.where(position_row == iota((items, rows), 0).astype(f32), 1.0, 0.0).astype(bf16)
    key_factor = dot(jnp.where(picked, 1.0, 0.0).astype(bf16), key_scale_ref[...])
    for h in range(heads):
        g = h // GROUP
        lanes = slice(h * HEAD_SIZE, (h + 1) * HEAD_SIZE)
        scaled = (
            query_ref[:, lanes].astype(f32) * key_factor[:, g * HEAD_SIZE : (g + 1) * HEAD_SIZE]
        ).astype(bf16)
        rows_f32[:, lanes] = dot(packer, scaled)
    rows_f32[:, query_width : query_width + kv_width] = dot(packer, new_key_ref[...])
    rows_f32[:, query_width + kv_width : meta_at] = dot(packer, new_value_ref[...])
    lane = iota((rows, META), 1)
    line = iota((rows, META), 0)
    task_high = jnp.floor(task_column * (1.0 / 128.0))
    task_low = task_column - task_high * 128.0
    facts = (
        jnp.where(lane == 0, slot_column + 1.0, 0.0)
        + jnp.where(lane == 1, length_column, 0.0)
        + jnp.where(lane == 2, task_high, 0.0)
        + jnp.where(lane == 3, task_low, 0.0)
    )
    shared = jnp.sum(
        jnp.where(lane == FIRST + line, owner_column, 0.0)
        + jnp.where(lane == FIRST + rows + line, slot_column, 0.0),
        axis=0,
        keepdims=True,
    )
    rows_f32[:, meta_at:] = dot(packer, facts.astype(bf16)) + shared
    for d in range(dp):
        send_rows[d] = rows_f32[d * capacity : (d + 1) * capacity, :].astype(bf16)

    pl.semaphore_wait(barrier, total - 1)

    def request_copy(k):
        return pltpu.make_async_remote_copy(
            src_ref=send_rows.at[lax.rem(me + k, dp)],
            dst_ref=recv_rows.at[me],
            send_sem=send_sem.at[0, k],
            recv_sem=recv_sem.at[0, k],
            device_id=(lax.rem(me + k, dp), part),
            device_id_type=MESH,
        )

    def request_arrival(k):
        return pltpu.make_async_remote_copy(
            src_ref=send_rows.at[0],
            dst_ref=recv_rows.at[lax.rem(me + dp - k, dp)],
            send_sem=send_sem.at[0, k],
            recv_sem=recv_sem.at[0, k],
            device_id=(lax.rem(me + k, dp), part),
            device_id_type=MESH,
        )

    for k in range(1, dp):
        request_copy(k).start()
    recv_rows[me] = send_rows[me]
    slot_query[...] = jnp.zeros_like(slot_query)
    for k in range(1, dp):
        request_arrival(k).wait_recv()

    for s in range(dp):
        rows_f32[s * capacity : (s + 1) * capacity, :] = recv_rows[s].astype(f32)
    facts_in = rows_f32[:, meta_at:]
    placing_row = to_row(facts_in[:, 0:1])
    placer = jnp.where(
        placing_row == iota((slots, items), 0).astype(f32) + 1.0, 1.0, 0.0
    ).astype(bf16)
    for h in range(heads):
        g = h // GROUP
        slot_query[:, h, g * HEAD_SIZE : (g + 1) * HEAD_SIZE] = dot(
            placer, rows_f32[:, h * HEAD_SIZE : (h + 1) * HEAD_SIZE].astype(bf16)
        )
    slot_small[0] = dot(placer, rows_f32[:, query_width : query_width + kv_width].astype(bf16))
    slot_small[1] = dot(placer, rows_f32[:, query_width + kv_width : meta_at].astype(bf16))
    slot_facts = dot(placer, facts_in.astype(bf16))
    slot_task = slot_facts[:, 2:3] * 128.0 + slot_facts[:, 3:4]
    slot_small[2] = dot(
        jnp.where(slot_task == iota((slots, task_total), 1).astype(f32), 1.0, 0.0).astype(bf16),
        value_scale_ref[...],
    )
    slot_length[...] = jnp.broadcast_to(slot_facts[:, 1:2], (slots, positions))

    fetches[0].wait()
    fetches[1].wait()
    inv_root = 1.0 / math.sqrt(HEAD_SIZE)
    key_line = iota((heads, positions), 1).astype(f32)

    def attend(s, carry):
        query = slot_query[s]
        one = pl.ds(s, 1)
        fresh_key = slot_small[0, one, :]
        fresh_value = slot_small[1, one, :]
        value_factor = slot_small[2, one, :]
        length = slot_length[one, :]
        scores = (
            lax.dot_general(
                query.astype(bf16), keys[s], (((1,), (1,)), ((), ())), preferred_element_type=f32
            )
            * inv_root
        )
        own = jnp.sum(query * fresh_key, axis=1, keepdims=True) * inv_root
        visible = key_line < length
        scores = jnp.where(visible, scores, masked_score)
        top = jnp.maximum(jnp.max(scores, axis=1, keepdims=True), own)
        weights = jnp.where(visible, jnp.exp(scores - top), 0.0)
        own_weight = jnp.exp(own - top)
        weight_sum = jnp.sum(weights, axis=1, keepdims=True) + own_weight
        blended = dot(weights.astype(bf16), values[s])
        blended = blended + own_weight.astype(bf16).astype(f32) * fresh_value
        attended = (blended / weight_sum).astype(bf16).astype(f32) * value_factor
        for g in range(kv_heads):
            slot_context[s, g * GROUP : (g + 1) * GROUP, :] = attended[
                g * GROUP : (g + 1) * GROUP, g * HEAD_SIZE : (g + 1) * HEAD_SIZE
            ]
        return carry

    lax.fori_loop(0, slots, attend, 0, unroll=4)
    for h in range(heads):
        context[me, :, h * HEAD_SIZE : (h + 1) * HEAD_SIZE] = slot_context[:, h, :].astype(bf16)

    def context_copy(k, source):
        return pltpu.make_async_remote_copy(
            src_ref=context.at[source],
            dst_ref=context.at[source],
            send_sem=send_sem.at[1, k],
            recv_sem=recv_sem.at[1, k],
            device_id=(lax.rem(me + k, dp), part),
            device_id_type=MESH,
        )

    for k in range(1, dp):
        context_copy(k, me).start()

    lane_r = iota((rows, META), 1)
    line_r = iota((rows, META), 0)
    for s in range(dp):
        fact_row = rows_f32[s * capacity : s * capacity + 1, meta_at:]
        owner_in = jnp.sum(
            jnp.where(lane_r == FIRST + line_r, fact_row, 0.0), axis=1, keepdims=True
        )
        slot_in = jnp.sum(
            jnp.where(lane_r == FIRST + rows + line_r, fact_row, 0.0), axis=1, keepdims=True
        )
        selector[s * rows : (s + 1) * rows, :] = jnp.where(
            owner_in * slots + slot_in == iota((rows, dp * slots), 1).astype(f32), 1.0, 0.0
        ).astype(bf16)
    fetches[2].wait()
    for k in range(1, dp):
        context_copy(k, lax.rem(me + dp - k, dp)).wait_recv()

    arranged = dot(selector[...], context[...].reshape(dp * slots, query_width)).astype(bf16)
    send_part[...] = dot(arranged, weight[...]).astype(bf16).reshape(dp, rows, columns)

    target_part = me // blocks
    place = lax.rem(me, blocks) * mp + part

    def part_copy(k):
        target = lax.rem(me + k, dp)
        return pltpu.make_async_remote_copy(
            src_ref=send_part.at[target],
            dst_ref=recv_part.at[place],
            send_sem=send_sem.at[2, k],
            recv_sem=recv_sem.at[2, place],
            device_id=(target, target_part),
            device_id_type=MESH,
        )

    def part_arrival(j):
        return pltpu.make_async_remote_copy(
            src_ref=send_part.at[0],
            dst_ref=recv_part.at[j],
            send_sem=send_sem.at[2, 0],
            recv_sem=recv_sem.at[2, j],
            device_id=(me, part),
            device_id_type=MESH,
        )

    for k in range(1, dp):
        part_copy(k).start()

    @pl.when(target_part != part)
    def _():
        part_copy(0).start()

    @pl.when(target_part == part)
    def _():
        recv_part[place] = send_part[me]

    for j in range(dp):
        own_block = (part * blocks + j // mp == me) & (part == j % mp)

        @pl.when(jnp.logical_not(own_block))
        def _():
            part_arrival(j).wait_recv()

    for e in range(blocks):
        summed = recv_part[e * mp].astype(f32)
        for j in range(1, mp):
            summed = summed + recv_part[e * mp + j].astype(f32)
        out_ref[:, e * columns : (e + 1) * columns] = summed.astype(bf16)

    for k in range(1, dp):
        request_copy(k).wait_send()
        context_copy(k, me).wait_send()
        part_copy(k).wait_send()

    @pl.when(target_part != part)
    def _():
        part_copy(0).wait_send()


def on_device(
    dp,
    mp,
    queries,
    incoming_key,
    incoming_value,
    key_cache,
    cached_values,
    task_key_scale,
    task_value_scale,
    out_weight,
    task_id,
    cached_length,
    task_owner,
    cache_slot,
):
    rows, query_width = queries.shape
    kv_width = incoming_key.shape[1]
    slots = key_cache.shape[0]
    capacity = 2 * rows // dp
    items = dp * capacity
    columns = out_weight.shape[1]
    row_width = query_width + 2 * kv_width + META
    heads = query_width // HEAD_SIZE
    vmem = pl.BlockSpec(memory_space=pltpu.VMEM)
    away = pl.BlockSpec(memory_space=pl.ANY)
    return pl.pallas_call(
        functools.partial(layer_kernel, dp, mp),
        out_shape=jax.ShapeDtypeStruct((rows, dp * columns // mp), bf16),
        in_specs=[vmem] * 9 + [away] * 3,
        out_specs=vmem,
        scratch_shapes=[
            pltpu.VMEM(key_cache.shape, bf16),
            pltpu.VMEM(cached_values.shape, bf16),
            pltpu.VMEM(out_weight.shape, bf16),
            pltpu.VMEM((items, row_width), f32),
            pltpu.VMEM((dp, capacity, row_width), bf16),
            pltpu.VMEM((dp, capacity, row_width), bf16),
            pltpu.VMEM((slots, heads, kv_width), f32),
            pltpu.VMEM((3, slots, kv_width), f32),
            pltpu.VMEM((slots, key_cache.shape[1]), f32),
            pltpu.VMEM((slots, heads, HEAD_SIZE), f32),
            pltpu.VMEM((dp, slots, query_width), bf16),
            pltpu.VMEM((dp * rows, dp * slots), bf16),
            pltpu.VMEM((dp, rows, columns), bf16),
            pltpu.VMEM((dp, rows, columns), bf16),
            pltpu.SemaphoreType.DMA((3,)),
            pltpu.SemaphoreType.DMA((3, dp)),
            pltpu.SemaphoreType.DMA((3, dp)),
        ],
        compiler_params=pltpu.CompilerParams(
            collective_id=0, has_side_effects=True, vmem_limit_bytes=60 * 1024 * 1024
        ),
    )(
        queries,
        incoming_key,
        incoming_value,
        task_key_scale,
        task_value_scale,
        task_id.reshape(1, -1),
        cached_length.reshape(1, -1),
        cache_slot.reshape(1, -1),
        task_owner.reshape(1, -1),
        key_cache,
        cached_values,
        out_weight,
    )


def solution(mesh):
    placed = (
        P("dp", "mp"),
        P("dp", "mp"),
        P("dp", "mp"),
        P("dp", None, "mp"),
        P("dp", None, "mp"),
        P(None, "mp"),
        P(None, "mp"),
        P("mp", "dp"),
        P("dp"),
        P("dp"),
        P(),
        P("dp"),
    )
    return jax.shard_map(
        functools.partial(on_device, mesh.shape["dp"], mesh.shape["mp"]),
        mesh=mesh,
        in_specs=placed,
        out_specs=P("dp", "mp"),
        check_vma=False,
    )
```

time: 167 us -> 58.5 us (0.35)
  the two profiles are of different devices: /device:TPU:0 before, /device:TPU:3 now
where the time goes in v2:
time: 58.5 us; the launch traced here: 58.3 us
  Pallas kernels  56.9 us (97%)
  local copies, waits for them, and re-layouts  1.47 us (3%)
    pallas_call x1, Pallas kernels, on_device(): pl.pallas_call(functools.partial(layer_kernel, dp, mp), out_shape=jax.Sha...  56.9 us
    unnamed x1, local copies, waits for them, and re-layouts  1.47 us

profile of v2, /device:TPU:3, one launch (start us, length us, event | category | flops | bytes accessed | tf_op | source)
XLA Modules:
  0.0 58.3 jit_solution(14801443200331678871)
XLA Ops:
  0.0 56.9 %shard_map.118 = bf16[16,2048]{1,0:T(8,128)(2,1)} custom-call(bf16[16,2048]{1,0:T(8,128)(2,1)} %query_ref.1, bf16[16,256]{1,0:T(8,128)(2,1)} %new_key_ref.1, bf16[16,256]{1,0:T(8,128)(2,1)} %new_value_ref.1, bf16[256,256]{1,0:T(8,128)(2,1)} %key_scale_ref.1, bf16[256,256]{1,0:T(8,128)(2,1)} %value_scale_ref.1, s32[1,16]{1,0:T(1,128)} %bitcast.5, ...), custom_call_target="tpu_custom_call" | custom-call | tf_op jit(solution)/shard_map/pallas_call | solution.py:366
  56.9 1.5 %copy.14 = bf16[16,2048]{1,0:T(8,128)(2,1)} copy(bf16[16,2048]{1,0:T(8,128)(2,1)} %shard_map.118) | data formatting | bytes 131072

commit v3 on v2

--- a/solution.py
+++ b/solution.py
@@ -14,6 +14,7 @@
 GROUP = QUERY_HEADS // KEY_VALUE_HEADS
 META = 128
 FIRST = 16
+CHUNKS = 4
 MESH = pl.DeviceIdType.MESH
 
 masked_score = -1e30
@@ -35,6 +36,11 @@
     n = column.shape[0]
     eye = iota((n, n), 0) == iota((n, n), 1)
     return jnp.sum(jnp.where(eye, column, 0.0), axis=0, keepdims=True)
+
+
+def factors(dp):
+    inner = 2 ** (int(math.log2(dp)) // 2)
+    return dp // inner, inner
 
 
 def dot(a, b):
@@ -74,6 +80,10 @@
     local_sem,
     send_sem,
     recv_sem,
+    along_send,
+    along_recv,
+    across_send,
+    across_recv,
 ):
     me = lax.axis_index("dp")
     part = lax.axis_index("mp")
@@ -88,6 +98,8 @@
     columns = weight.shape[1]
     blocks = dp // mp
     meta_at = query_width + 2 * kv_width
+    chunks, chunk = context.shape[1:3]
+    outer, inner = factors(dp)
 
     total = dp * mp
     here = me * mp + part
@@ -242,22 +254,49 @@
             ]
         return carry
 
-    lax.fori_loop(0, slots, attend, 0, unroll=4)
-    for h in range(heads):
-        context[me, :, h * HEAD_SIZE : (h + 1) * HEAD_SIZE] = slot_context[:, h, :].astype(bf16)
-
-    def context_copy(k, source):
-        return pltpu.make_async_remote_copy(
-            src_ref=context.at[source],
-            dst_ref=context.at[source],
-            send_sem=send_sem.at[1, k],
-            recv_sem=recv_sem.at[1, k],
-            device_id=(lax.rem(me + k, dp), part),
-            device_id_type=MESH,
-        )
-
-    for k in range(1, dp):
-        context_copy(k, me).start()
+    column, line_in = me // inner, lax.rem(me, inner)
+
+    def source_of(k):
+        return lax.rem(column + outer - k, outer) * inner + line_in
+
+    def along_copy(k, c, source):
+        return pltpu.make_async_remote_copy(
+            src_ref=context.at[source, c],
+            dst_ref=context.at[source, c],
+            send_sem=along_send.at[k, c],
+            recv_sem=along_recv.at[k, c],
+            device_id=(lax.rem(column + k, outer) * inner + line_in, part),
+            device_id_type=MESH,
+        )
+
+    def across_copy(k, j, c, source):
+        return pltpu.make_async_remote_copy(
+            src_ref=context.at[source, c],
+            dst_ref=context.at[source, c],
+            send_sem=across_send.at[k, j, c],
+            recv_sem=across_recv.at[k, j, c],
+            device_id=(column * inner + lax.rem(line_in + j, inner), part),
+            device_id_type=MESH,
+        )
+
+    def forward(c):
+        for k in range(1, outer):
+            along_copy(k, c, source_of(k)).wait_recv()
+            for j in range(1, inner):
+                across_copy(k, j, c, source_of(k)).start()
+
+    for c in range(chunks):
+        lax.fori_loop(c * chunk, (c + 1) * chunk, attend, 0, unroll=min(chunk, 8))
+        for h in range(heads):
+            context[me, c, :, h * HEAD_SIZE : (h + 1) * HEAD_SIZE] = slot_context[
+                c * chunk : (c + 1) * chunk, h, :
+            ].astype(bf16)
+        for k in range(outer - 1, 0, -1):
+            along_copy(k, c, me).start()
+        for j in range(1, inner):
+            across_copy(0, j, c, me).start()
+        if c > 0:
+            forward(c - 1)
 
     lane_r = iota((rows, META), 1)
     line_r = iota((rows, META), 0)
@@ -273,8 +312,14 @@
             owner_in * slots + slot_in == iota((rows, dp * slots), 1).astype(f32), 1.0, 0.0
         ).astype(bf16)
     fetches[2].wait()
-    for k in range(1, dp):
-        context_copy(k, lax.rem(me + dp - k, dp)).wait_recv()
+    forward(chunks - 1)
+    for c in range(chunks):
+        for k in range(outer):
+            for j in range(1, inner):
+                source = lax.rem(column + outer - k, outer) * inner + lax.rem(
+                    line_in + inner - j, inner
+                )
+                across_copy(k, j, c, source).wait_recv()
 
     arranged = dot(selector[...], context[...].reshape(dp * slots, query_width)).astype(bf16)
     send_part[...] = dot(arranged, weight[...]).astype(bf16).reshape(dp, rows, columns)
@@ -329,8 +374,14 @@
 
     for k in range(1, dp):
         request_copy(k).wait_send()
-        context_copy(k, me).wait_send()
         part_copy(k).wait_send()
+
+    for c in range(chunks):
+        for k in range(outer):
+            if k > 0:
+                along_copy(k, c, me).wait_send()
+            for j in range(1, inner):
+                across_copy(k, j, c, source_of(k)).wait_send()
 
     @pl.when(target_part != part)
     def _():
@@ -361,6 +412,7 @@
     columns = out_weight.shape[1]
     row_width = query_width + 2 * kv_width + META
     heads = query_width // HEAD_SIZE
+    outer, inner = factors(dp)
     vmem = pl.BlockSpec(memory_space=pltpu.VMEM)
     away = pl.BlockSpec(memory_space=pl.ANY)
     return pl.pallas_call(
@@ -379,13 +431,17 @@
             pltpu.VMEM((3, slots, kv_width), f32),
             pltpu.VMEM((slots, key_cache.shape[1]), f32),
             pltpu.VMEM((slots, heads, HEAD_SIZE), f32),
-            pltpu.VMEM((dp, slots, query_width), bf16),
+            pltpu.VMEM((dp, CHUNKS, slots // CHUNKS, query_width), bf16),
             pltpu.VMEM((dp * rows, dp * slots), bf16),
             pltpu.VMEM((dp, rows, columns), bf16),
             pltpu.VMEM((dp, rows, columns), bf16),
             pltpu.SemaphoreType.DMA((3,)),
             pltpu.SemaphoreType.DMA((3, dp)),
             pltpu.SemaphoreType.DMA((3, dp)),
+            pltpu.SemaphoreType.DMA((outer, CHUNKS)),
+            pltpu.SemaphoreType.DMA((outer, CHUNKS)),
+            pltpu.SemaphoreType.DMA((outer, inner, CHUNKS)),
+            pltpu.SemaphoreType.DMA((outer, inner, CHUNKS)),
         ],
         compiler_params=pltpu.CompilerParams(
             collective_id=0, has_side_effects=True, vmem_limit_bytes=60 * 1024 * 1024

time: 58.5 us -> 44.2 us (0.76)
  the two profiles are of different devices: /device:TPU:3 before, /device:TPU:0 now
where the time goes in v3:
time: 44.2 us; the launch traced here: 44 us
  Pallas kernels  42.5 us (96%)
  local copies, waits for them, and re-layouts  1.47 us (3%)
    pallas_call x1, Pallas kernels, on_device(): pl.pallas_call(functools.partial(layer_kernel, dp, mp), out_shape=jax.Sha...  42.5 us
    unnamed x1, local copies, waits for them, and re-layouts  1.47 us

profile of v3, /device:TPU:0, one launch (start us, length us, event | category | flops | bytes accessed | tf_op | source)
XLA Modules:
  0.0 44.0 jit_solution(5363908289917555441)
XLA Ops:
  0.0 42.5 %shard_map.118 = bf16[16,2048]{1,0:T(8,128)(2,1)} custom-call(bf16[16,2048]{1,0:T(8,128)(2,1)} %query_ref.1, bf16[16,256]{1,0:T(8,128)(2,1)} %new_key_ref.1, bf16[16,256]{1,0:T(8,128)(2,1)} %new_value_ref.1, bf16[256,256]{1,0:T(8,128)(2,1)} %key_scale_ref.1, bf16[256,256]{1,0:T(8,128)(2,1)} %value_scale_ref.1, s32[1,16]{1,0:T(1,128)} %bitcast.5, ...), custom_call_target="tpu_custom_call" | custom-call | tf_op jit(solution)/shard_map/pallas_call | solution.py:418
  42.5 1.5 %copy.14 = bf16[16,2048]{1,0:T(8,128)(2,1)} copy(bf16[16,2048]{1,0:T(8,128)(2,1)} %shard_map.118) | data formatting | bytes 131072

commit v4 on v3

--- a/solution.py
+++ b/solution.py
@@ -14,6 +14,7 @@
 GROUP = QUERY_HEADS // KEY_VALUE_HEADS
 META = 128
 FIRST = 16
+TOGETHER = 8
 CHUNKS = 4
 MESH = pl.DeviceIdType.MESH
 
@@ -225,33 +226,44 @@
     inv_root = 1.0 / math.sqrt(HEAD_SIZE)
     key_line = iota((heads, positions), 1).astype(f32)
 
-    def attend(s, carry):
-        query = slot_query[s]
-        one = pl.ds(s, 1)
-        fresh_key = slot_small[0, one, :]
-        fresh_value = slot_small[1, one, :]
-        value_factor = slot_small[2, one, :]
-        length = slot_length[one, :]
-        scores = (
-            lax.dot_general(
-                query.astype(bf16), keys[s], (((1,), (1,)), ((), ())), preferred_element_type=f32
+    def attend(n, carry):
+        picks = [n * TOGETHER + i for i in range(TOGETHER)]
+        scores, owns, weights, own_weights, sums, tops = [], [], [], [], [], []
+        for s in picks:
+            scores.append(
+                lax.dot_general(
+                    slot_query[s].astype(bf16),
+                    keys[s],
+                    (((1,), (1,)), ((), ())),
+                    preferred_element_type=f32,
+                )
+                * inv_root
             )
-            * inv_root
-        )
-        own = jnp.sum(query * fresh_key, axis=1, keepdims=True) * inv_root
-        visible = key_line < length
-        scores = jnp.where(visible, scores, masked_score)
-        top = jnp.maximum(jnp.max(scores, axis=1, keepdims=True), own)
-        weights = jnp.where(visible, jnp.exp(scores - top), 0.0)
-        own_weight = jnp.exp(own - top)
-        weight_sum = jnp.sum(weights, axis=1, keepdims=True) + own_weight
-        blended = dot(weights.astype(bf16), values[s])
-        blended = blended + own_weight.astype(bf16).astype(f32) * fresh_value
-        attended = (blended / weight_sum).astype(bf16).astype(f32) * value_factor
-        for g in range(kv_heads):
-            slot_context[s, g * GROUP : (g + 1) * GROUP, :] = attended[
-                g * GROUP : (g + 1) * GROUP, g * HEAD_SIZE : (g + 1) * HEAD_SIZE
-            ]
+        for s in picks:
+            owns.append(
+                jnp.sum(slot_query[s] * slot_small[0, pl.ds(s, 1), :], axis=1, keepdims=True)
+                * inv_root
+            )
+        for i, s in enumerate(picks):
+            visible = key_line < slot_length[pl.ds(s, 1), :]
+            shown = jnp.where(visible, scores[i], masked_score)
+            tops.append(jnp.maximum(jnp.max(shown, axis=1, keepdims=True), owns[i]))
+        for i, s in enumerate(picks):
+            visible = key_line < slot_length[pl.ds(s, 1), :]
+            shown = jnp.where(visible, scores[i], masked_score)
+            weights.append(jnp.where(visible, jnp.exp(shown - tops[i]), 0.0))
+            own_weights.append(jnp.exp(owns[i] - tops[i]))
+        blends = [dot(weights[i].astype(bf16), values[s]) for i, s in enumerate(picks)]
+        for i in range(TOGETHER):
+            sums.append(jnp.sum(weights[i], axis=1, keepdims=True) + own_weights[i])
+        for i, s in enumerate(picks):
+            one = pl.ds(s, 1)
+            blended = blends[i] + own_weights[i].astype(bf16).astype(f32) * slot_small[1, one, :]
+            attended = (blended / sums[i]).astype(bf16).astype(f32) * slot_small[2, one, :]
+            for g in range(kv_heads):
+                slot_context[s, g * GROUP : (g + 1) * GROUP, :] = attended[
+                    g * GROUP : (g + 1) * GROUP, g * HEAD_SIZE : (g + 1) * HEAD_SIZE
+                ]
         return carry
 
     column, line_in = me // inner, lax.rem(me, inner)
@@ -286,7 +298,7 @@
                 across_copy(k, j, c, source_of(k)).start()
 
     for c in range(chunks):
-        lax.fori_loop(c * chunk, (c + 1) * chunk, attend, 0, unroll=min(chunk, 8))
+        lax.fori_loop(c * chunk // TOGETHER, (c + 1) * chunk // TOGETHER, attend, 0)
         for h in range(heads):
             context[me, c, :, h * HEAD_SIZE : (h + 1) * HEAD_SIZE] = slot_context[
                 c * chunk : (c + 1) * chunk, h, :

time: 44.2 us -> 40.8 us (0.923)
  Pallas kernels: 42.5 us -> 39.1 us
    pallas_call x1, Pallas kernels: 42.5 us -> 39.1 us  [on_device(): pl.pallas_call(functools.partial(layer_kernel, dp, mp), out_shape=jax.Sha...]
where the time goes in v4:
time: 40.8 us; the launch traced here: 40.6 us
  Pallas kernels  39.1 us (96%)
  local copies, waits for them, and re-layouts  1.47 us (4%)
    pallas_call x1, Pallas kernels, on_device(): pl.pallas_call(functools.partial(layer_kernel, dp, mp), out_shape=jax.Sha...  39.1 us
    unnamed x1, local copies, waits for them, and re-layouts  1.47 us

profile of v4, /device:TPU:0, one launch (start us, length us, event | category | flops | bytes accessed | tf_op | source)
XLA Modules:
  0.0 40.6 jit_solution(12661803052259685337)
XLA Ops:
  0.0 39.1 %shard_map.118 = bf16[16,2048]{1,0:T(8,128)(2,1)} custom-call(bf16[16,2048]{1,0:T(8,128)(2,1)} %query_ref.1, bf16[16,256]{1,0:T(8,128)(2,1)} %new_key_ref.1, bf16[16,256]{1,0:T(8,128)(2,1)} %new_value_ref.1, bf16[256,256]{1,0:T(8,128)(2,1)} %key_scale_ref.1, bf16[256,256]{1,0:T(8,128)(2,1)} %value_scale_ref.1, s32[1,16]{1,0:T(1,128)} %bitcast.5, ...), custom_call_target="tpu_custom_call" | custom-call | tf_op jit(solution)/shard_map/pallas_call | solution.py:430
  39.1 1.5 %copy.14 = bf16[16,2048]{1,0:T(8,128)(2,1)} copy(bf16[16,2048]{1,0:T(8,128)(2,1)} %shard_map.118) | data formatting | bytes 131072

commit v5 on v4

--- a/solution.py
+++ b/solution.py
@@ -292,7 +292,7 @@
         )
 
     def forward(c):
-        for k in range(1, outer):
+        for k in (outer - 1, *range(1, outer - 1)):
             along_copy(k, c, source_of(k)).wait_recv()
             for j in range(1, inner):
                 across_copy(k, j, c, source_of(k)).start()
@@ -303,7 +303,7 @@
             context[me, c, :, h * HEAD_SIZE : (h + 1) * HEAD_SIZE] = slot_context[
                 c * chunk : (c + 1) * chunk, h, :
             ].astype(bf16)
-        for k in range(outer - 1, 0, -1):
+        for k in range(1, outer):
             along_copy(k, c, me).start()
         for j in range(1, inner):
             across_copy(0, j, c, me).start()

time: 40.8 us -> 40.1 us (0.983); the launches traced: 40.6 us -> 39.4 us
  Pallas kernels: 39.1 us -> 38 us
    pallas_call x1, Pallas kernels: 39.1 us -> 38 us  [on_device(): pl.pallas_call(functools.partial(layer_kernel, dp, mp), out_shape=jax.Sha...]
where the time goes in v5:
time: 40.1 us; the launch traced here: 39.4 us
  Pallas kernels  38 us (95%)
  local copies, waits for them, and re-layouts  1.47 us (4%)
    pallas_call x1, Pallas kernels, on_device(): pl.pallas_call(functools.partial(layer_kernel, dp, mp), out_shape=jax.Sha...  38 us
    unnamed x1, local copies, waits for them, and re-layouts  1.47 us

profile of v5, /device:TPU:0, one launch (start us, length us, event | category | flops | bytes accessed | tf_op | source)
XLA Modules:
  0.0 39.4 jit_solution(15318382825774511149)
XLA Ops:
  0.0 38.0 %shard_map.118 = bf16[16,2048]{1,0:T(8,128)(2,1)} custom-call(bf16[16,2048]{1,0:T(8,128)(2,1)} %query_ref.1, bf16[16,256]{1,0:T(8,128)(2,1)} %new_key_ref.1, bf16[16,256]{1,0:T(8,128)(2,1)} %new_value_ref.1, bf16[256,256]{1,0:T(8,128)(2,1)} %key_scale_ref.1, bf16[256,256]{1,0:T(8,128)(2,1)} %value_scale_ref.1, s32[1,16]{1,0:T(1,128)} %bitcast.5, ...), custom_call_target="tpu_custom_call" | custom-call | tf_op jit(solution)/shard_map/pallas_call | solution.py:430
  38.0 1.5 %copy.14 = bf16[16,2048]{1,0:T(8,128)(2,1)} copy(bf16[16,2048]{1,0:T(8,128)(2,1)} %shard_map.118) | data formatting | bytes 131072
